TPU v7x, 32 devices: a whole 2x2x4 slice. The times are simulated.
32 devices in a mesh: row: 4 (over x, core), col: 8 (over z, y).
Axes of the slice: x: 2, y: 2, z: 4, core: 2. Of those that a mesh axis runs over, the one named last changes fastest.
Arguments:
- picture_embedding_matrix: bfloat16 [2048, 1152], P(('row', 'col')), may hold values from -0.19921875 to 0.19921875
- caption_embedding_matrix: bfloat16 [2048, 1152], P(('row', 'col')), may hold values from -0.19921875 to 0.19921875
- sharpness_scale: float32 [1], replicated, may hold values from 4 to 12
- additive_shift: float32 [1], replicated, may hold values from -4 to -2
Outputs:
- grad_images: float32 [2048, 1152], P(('row', 'col'))
- grad_texts: float32 [2048, 1152], P(('row', 'col'))
- image_loss: float32 [2048], P(('row', 'col'))
All inputs are finite; a program needn't handle non-finite values.
Results may differ from a plain program's by a relative error of at most 0.0053.
Values may be sent and summed in bfloat16 or wider, within the bound.
A program may use at most 128 MiB of HBM per device.

v0:
```python
import functools

import jax
import jax.numpy as jnp
from jax import lax
from jax.experimental import pallas as pl
from jax.experimental.pallas import tpu as pltpu
from jax.sharding import PartitionSpec as P

EPS = 1e-06
MESH = pl.DeviceIdType.MESH
PIECES = 2
TILE = 256


def bits_of(n):
    return n.bit_length() - 1


def groups(n_row, n_col):
    row_bits, col_bits = bits_of(n_row), bits_of(n_col)
    take = min(max((row_bits + col_bits + 1) // 2 - row_bits, 0), col_bits)
    choice = [b for b in range(1, col_bits)] + [0] * (col_bits > 0)
    mine, rest = choice[:take], choice[take:]
    images = [("col", b) for b in sorted(mine, reverse=True)]
    images += [("row", b) for b in reversed(range(row_bits))]
    texts = [("col", b) for b in sorted(rest, reverse=True)]
    return images, texts


def flip(index, bit):
    step = 2**bit
    return index + step * (1 - 2 * lax.rem(lax.div(index, step), 2))


def peer_of(dims, mask):
    at = {"row": lax.axis_index("row"), "col": lax.axis_index("col")}
    for j, (axis, bit) in enumerate(dims):
        if mask >> j & 1:
            at[axis] = flip(at[axis], bit)
    return (at["row"], at["col"])


def top(slot):
    return slot.bit_length() - 1


def inverse_norm(values):
    return lax.rsqrt(jnp.sum(values * values, axis=-1, keepdims=True) + EPS)


def tiles(count, body):
    if count <= 4:
        for t in range(count):
            body(t)
    else:
        lax.fori_loop(0, count, lambda t, _: (body(t), 0)[1], 0)


def kernel(
    dims,
    img_hbm,
    txt_hbm,
    scale_ref,
    shift_ref,
    gi_ref,
    gt_ref,
    loss_ref,
    own_img,
    own_txt,
    load,
    img_raw,
    txt_raw,
    img_n,
    txt_n,
    coef,
    acc_img,
    acc_txt,
    out_img,
    out_txt,
    in_img,
    in_txt,
    loss_sum,
    loss_out,
    loss_in,
    gs_img,
    gr_img,
    gs_txt,
    gr_txt,
    ss_img,
    sr_img,
    ss_txt,
    sr_txt,
    ls,
    lr,
):
    rows, _ = img_hbm.shape
    part = rows // PIECES
    size = {"i": 2 ** len(dims["i"]), "t": 2 ** len(dims["t"])}
    own = {"i": own_img, "t": own_txt}
    raw = {"i": img_raw, "t": txt_raw}
    unit = {"i": img_n, "t": txt_n}
    acc = {"i": acc_img, "t": acc_txt}
    out = {"i": out_img, "t": out_txt}
    into = {"i": in_img, "t": in_txt}
    g_sems = {"i": (gs_img, gr_img), "t": (gs_txt, gr_txt)}
    s_sems = {"i": (ss_img, sr_img), "t": (ss_txt, sr_txt)}
    sent = []

    peers = [peer_of(dims["i"], m) for m in range(1, size["i"])]
    peers += [peer_of(dims["t"], 2**j) for j in range(len(dims["t"]))]
    barrier = pltpu.get_barrier_semaphore()
    for peer in peers:
        pl.semaphore_signal(barrier, inc=1, device_id=peer, device_id_type=MESH)
    loads = [
        pltpu.make_async_copy(source, target, load.at[n])
        for n, (source, target) in enumerate(
            [
                (txt_hbm, own_txt),
                (img_hbm, own_img),
            ]
        )
    ]
    for copy in loads:
        copy.start()
    for copy in loads:
        copy.wait()
    pl.semaphore_wait(barrier, len(peers))

    gather = {}

    def spread(g, slot, j, p):
        to = slot | 1 << j
        piece = pl.ds(p * part, part)
        source = own[g].at[piece] if slot == 0 else raw[g].at[slot, piece]
        copy = pltpu.make_async_remote_copy(
            src_ref=source,
            dst_ref=raw[g].at[to, piece],
            send_sem=g_sems[g][0].at[to, p],
            recv_sem=g_sems[g][1].at[to, p],
            device_id=peer_of(dims[g], 1 << j),
            device_id_type=MESH,
        )
        copy.start()
        gather[g, to, p] = copy
        sent.append(copy)

    for p in range(PIECES):
        for j in range(max(len(dims["i"]), len(dims["t"]))):
            for g in ("i", "t"):
                if j < len(dims[g]):
                    spread(g, 0, j, p)

    def normalize(g, slot):
        values = (own[g][...] if slot == 0 else raw[g][slot]).astype(jnp.float32)
        unit[g][slot * rows : (slot + 1) * rows, :] = (values * inverse_norm(values)).astype(
            jnp.bfloat16
        )

    normalize("i", 0)
    normalize("t", 0)
    levels = max(len(dims["i"]), len(dims["t"]))
    for level in range(1, levels + 1):
        slots = [
            (g, s)
            for s in reversed(range(1, max(size.values())))
            for g in ("i", "t")
            if s < size[g] and s.bit_count() == level
        ]
        for p in range(PIECES):
            for g, s in slots:
                gather[g, s, p].wait_recv()
                for j in range(top(s) + 1, len(dims[g])):
                    spread(g, s, j, p)
                if p == PIECES - 1:
                    normalize(g, s)

    scale, shift = scale_ref[0], shift_ref[0]
    n_img, n_txt = size["i"] * rows, size["t"] * rows
    t_img, t_txt = min(TILE, n_img), min(TILE, n_txt)
    loss_sum[...] = jnp.zeros_like(loss_sum)

    def logits(t):
        if isinstance(t, int):
            at_txt, at_img = t // (n_img // t_img) * t_txt, t % (n_img // t_img) * t_img
        else:
            at_txt = pl.multiple_of(lax.div(t, n_img // t_img) * t_txt, t_txt)
            at_img = pl.multiple_of(lax.rem(t, n_img // t_img) * t_img, t_img)
        here_txt, here_img = pl.ds(at_txt, t_txt), pl.ds(at_img, t_img)
        value = lax.dot_general(
            txt_n[here_txt, :],
            img_n[here_img, :],
            (((1,), (1,)), ((), ())),
            preferred_element_type=jnp.float32,
        )
        value = value * scale + shift
        weight = scale
        if not isinstance(t, int) or t == 0:
            a = lax.broadcasted_iota(jnp.int32, value.shape, 0) + at_txt
            b = lax.broadcasted_iota(jnp.int32, value.shape, 1) + at_img
            match = (a == b) & (a < rows)
            value = jnp.where(match, -value, value)
            weight = jnp.where(match, -scale, scale)
        e = jnp.exp(value)
        loss_sum[:, here_img] += jnp.sum(jnp.log1p(e), axis=0, keepdims=True)
        coef[here_txt, here_img] = (weight * (e / (1.0 + e))).astype(jnp.bfloat16)

    tiles((n_txt // t_txt) * (n_img // t_img), logits)

    losses = []
    for s in range(1, size["i"]):
        loss_out[s] = loss_sum[:, s * rows : (s + 1) * rows]
        copy = pltpu.make_async_remote_copy(
            src_ref=loss_out.at[s],
            dst_ref=loss_in.at[s],
            send_sem=ls.at[s],
            recv_sem=lr.at[s],
            device_id=peer_of(dims["i"], s),
            device_id_type=MESH,
        )
        copy.start()
        losses.append(copy)
        sent.append(copy)

    scatter = {}

    def pass_on(g, s, p):
        piece = pl.ds(p * part, part)
        copy = pltpu.make_async_remote_copy(
            src_ref=out[g].at[s, piece],
            dst_ref=into[g].at[s, piece],
            send_sem=s_sems[g][0].at[s, p],
            recv_sem=s_sems[g][1].at[s, p],
            device_id=peer_of(dims[g], 1 << top(s)),
            device_id_type=MESH,
        )
        copy.start()
        scatter[g, s, p] = copy
        sent.append(copy)

    def product(g, first, count):
        here = pl.ds(first * rows, count * rows)
        if not isinstance(first, int):
            here = pl.ds(pl.multiple_of(first * rows, count * rows), count * rows)
        if g == "t":
            return jnp.dot(coef[here, :], img_n[...], preferred_element_type=jnp.float32)
        return lax.dot_general(
            coef[:, here], txt_n[...], (((0,), (0,)), ((), ())), preferred_element_type=jnp.float32
        )

    def grads(g, upper):
        half = size[g] // 2
        base = half if upper else 0
        step = min(half, TILE // rows)

        def body(t):
            first = base + t * step
            value = product(g, first, step)
            if upper:
                out[g][pl.ds(first, step)] = value.reshape(step, rows, -1).astype(jnp.bfloat16)
            else:
                acc[g][pl.ds(first, step)] = value.reshape(step, rows, -1)

        tiles(half // step, body)
        if upper:
            for s in reversed(range(half, size[g])):
                for p in range(PIECES):
                    pass_on(g, s, p)

    grads("t", True)
    grads("i", True)
    grads("i", False)
    grads("t", False)

    def total(g, k, p):
        piece = pl.ds(p * part, part)
        value = acc[g][k, piece]
        for j in reversed(range(top(k) + 1 if k else 0, len(dims[g]))):
            scatter[g, k | 1 << j, p].wait_recv()
            value = value + into[g][k | 1 << j, piece].astype(jnp.float32)
        return value

    order = sorted(
        [(k.bit_length() - len(dims[g]), g, k) for g in ("i", "t") for k in range(1, size[g] // 2)],
        key=lambda item: (-item[0], item[1] != "i", -item[2]),
    )
    for _, g, k in order:
        for p in range(PIECES):
            out[g][k, pl.ds(p * part, part)] = total(g, k, p).astype(jnp.bfloat16)
            pass_on(g, k, p)

    value = loss_sum[:, :rows]
    for s, copy in enumerate(losses, 1):
        copy.wait_recv()
        value = value + loss_in[s]
    loss_ref[...] = value

    for g, result in (("i", gi_ref), ("t", gt_ref)):
        for p in range(PIECES):
            piece = pl.ds(p * part, part)
            grad = total(g, 0, p)
            values = own[g][piece].astype(jnp.float32)
            inverse = inverse_norm(values)
            unit_row = values * inverse
            along = jnp.sum(unit_row * grad, axis=-1, keepdims=True)
            result[piece, :] = inverse * (grad - unit_row * along)

    for copy in sent:
        copy.wait_send()


def hand_out(gi_from, gt_from, loss_from, gi_ref, gt_ref, loss_ref, sems):
    pairs = ((gi_from, gi_ref), (gt_from, gt_ref), (loss_from, loss_ref))
    copies = [pltpu.make_async_copy(a, b, sems.at[n]) for n, (a, b) in enumerate(pairs)]
    for copy in copies:
        copy.start()
    for copy in copies:
        copy.wait()


def on_device(n_row, n_col, images, texts, scale, shift):
    rows, width = images.shape
    dims = dict(zip("it", groups(n_row, n_col)))
    a, b = 2 ** len(dims["i"]), 2 ** len(dims["t"])
    vmem = pl.BlockSpec(memory_space=pltpu.VMEM)
    smem = pl.BlockSpec(memory_space=pltpu.SMEM)
    hbm = pl.BlockSpec(memory_space=pl.ANY)
    f32, bf16 = jnp.float32, jnp.bfloat16
    sums = pl.pallas_call(
        functools.partial(kernel, dims),
        out_shape=(
            pltpu.VMEM((rows, width), f32),
            pltpu.VMEM((rows, width), f32),
            pltpu.VMEM((1, rows), f32),
        ),
        in_specs=[hbm, hbm, smem, smem],
        out_specs=(vmem, vmem, vmem),
        scratch_shapes=[
            pltpu.VMEM((rows, width), bf16),
            pltpu.VMEM((rows, width), bf16),
            pltpu.SemaphoreType.DMA((2,)),
            pltpu.VMEM((a, rows, width), bf16),
            pltpu.VMEM((b, rows, width), bf16),
            pltpu.VMEM((a * rows, width), bf16),
            pltpu.VMEM((b * rows, width), bf16),
            pltpu.VMEM((b * rows, a * rows), bf16),
            pltpu.VMEM((a // 2, rows, width), f32),
            pltpu.VMEM((b // 2, rows, width), f32),
            pltpu.VMEM((a, rows, width), bf16),
            pltpu.VMEM((b, rows, width), bf16),
            pltpu.VMEM((a, rows, width), bf16),
            pltpu.VMEM((b, rows, width), bf16),
            pltpu.VMEM((1, a * rows), f32),
            pltpu.VMEM((a, 1, rows), f32),
            pltpu.VMEM((a, 1, rows), f32),
        ]
        + [pltpu.SemaphoreType.DMA((n, PIECES)) for n in (a, a, b, b, a, a, b, b)]
        + [pltpu.SemaphoreType.DMA((a,)), pltpu.SemaphoreType.DMA((a,))],
        compiler_params=pltpu.CompilerParams(collective_id=0, has_side_effects=True),
    )(*[pltpu.with_memory_space_constraint(x, pltpu.HBM) for x in (images, texts)], scale, shift)
    gi, gt, loss = pl.pallas_call(
        hand_out,
        out_shape=(
            jax.ShapeDtypeStruct((rows, width), f32),
            jax.ShapeDtypeStruct((rows, width), f32),
            jax.ShapeDtypeStruct((1, rows), f32),
        ),
        in_specs=[hbm] * 3,
        out_specs=(hbm, hbm, hbm),
        scratch_shapes=[pltpu.SemaphoreType.DMA((3,))],
    )(*[pltpu.with_memory_space_constraint(x, pltpu.VMEM) for x in sums])
    return gi, gt, loss.reshape(rows)


def solution(mesh):
    placed = (P(("row", "col"), None), P(("row", "col"), None), P(), P())
    return jax.shard_map(
        functools.partial(on_device, mesh.shape["row"], mesh.shape["col"]),
        mesh=mesh,
        in_specs=placed,
        out_specs=(P(("row", "col"), None), P(("row", "col"), None), P(("row", "col"))),
        check_vma=False,
    )
```

profile of v0, /device:TPU:0, one launch (start us, length us, event | category | flops | bytes accessed | tf_op | source)
XLA Modules:
  0.0 34.7 jit_solution(2315137283548969225)
XLA Ops:
  1.9 32.0 %shard_map.67 = (f32[64,1152]{1,0:T(8,128)S(1)}, f32[64,1152]{1,0:T(8,128)S(1)}, f32[1,64]{1,0:T(1,128)S(1)}) custom-call(bf16[64,1152]{1,0:T(8,128)(2,1)} %img_hbm.1, bf16[64,1152]{1,0:T(8,128)(2,1)} %txt_hbm.1, f32[1]{0:T(128)S(6)} %copy.7.scale_ref, f32[1]{0:T(128)S(6)} %copy.8.shift_ref), custom_call_target="tpu_custom_call" | custom-call | tf_op jit(solution)/shard_map/pallas_call | solution.py:329
  33.9 0.8 %shard_map.68 = (f32[64,1152]{1,0:T(8,128)}, f32[64,1152]{1,0:T(8,128)}, f32[1,64]{1,0:T(1,128)}) custom-call(f32[64,1152]{1,0:T(8,128)S(1)} %get-tuple-element.9.gi_from, f32[64,1152]{1,0:T(8,128)S(1)} %get-tuple-element.10.gt_from, f32[1,64]{1,0:T(1,128)S(1)} %get-tuple-element.11.loss_from), custom_call_target="tpu_custom_call" | custom-call | tf_op jit(solution)/shard_map/pallas_call | solution.py:361
where the time goes:
time: 34.9 us; the launch traced here: 34.7 us
  Pallas kernels  32.8 us (94%)
  between operations  1.93 us (6%)
    pallas_call x1, Pallas kernels, on_device(): pl.pallas_call(functools.partial(kernel, dims), out_shape=(pltpu.VMEM((ro...  32 us
    pallas_call x1, Pallas kernels, on_device(): pl.pallas_call(hand_out, out_shape=(jax.ShapeDtypeStruct((rows, width), f...  0.84 us

commit v1 on v0

v1 whole, which is shorter than its diff:
```python
import functools

import jax
import jax.numpy as jnp
from jax import lax
from jax.experimental import pallas as pl
from jax.experimental.pallas import tpu as pltpu
from jax.sharding import PartitionSpec as P

EPS = 1e-06
MESH = pl.DeviceIdType.MESH
CORE = ("row", 0)
TILE = 256


def bits_of(n):
    return n.bit_length() - 1


def groups(n_row, n_col):
    row_bits, col_bits = bits_of(n_row), bits_of(n_col)
    take = min(max((row_bits + col_bits + 1) // 2 - row_bits, 0), col_bits)
    choice = [b for b in range(1, col_bits)] + [0] * (col_bits > 0)
    mine, rest = choice[:take], choice[take:]
    images = [("col", b) for b in sorted(mine, reverse=True)]
    images += [("row", b) for b in reversed(range(1, row_bits))]
    texts = [("col", b) for b in sorted(rest, reverse=True)]
    return images, texts


def flip(index, bit):
    step = 2**bit
    return index + step * (1 - 2 * lax.rem(lax.div(index, step), 2))


def across(axis, bit):
    at = {"row": lax.axis_index("row"), "col": lax.axis_index("col")}
    at[axis] = flip(at[axis], bit)
    return (at["row"], at["col"])


def top(slot):
    return slot.bit_length() - 1


def pieces_of(rows):
    quarter = rows // 4
    return [(0, quarter), (quarter, rows - 2 * quarter), (rows - quarter, quarter)]


def inverse_norm(values):
    return lax.rsqrt(jnp.sum(values * values, axis=-1, keepdims=True) + EPS)


def tiles(count, body):
    if count <= 4:
        for t in range(count):
            body(t)
    else:
        lax.fori_loop(0, count, lambda t, _: (body(t), 0)[1], 0)


def kernel(
    dims,
    img_hbm,
    txt_hbm,
    scale_ref,
    shift_ref,
    gi_ref,
    gt_ref,
    loss_ref,
    raw_img,
    raw_txt,
    unit_img,
    unit_txt,
    coef_img,
    coef_txt,
    acc_img,
    acc_txt,
    out_img,
    out_txt,
    in_img,
    in_txt,
    loss_lanes,
    loss_acc,
    loss_out,
    loss_in,
    load,
    sends,
    gr_img,
    gr_txt,
    cr_img,
    cr_txt,
    sr_img,
    sr_txt,
    lr,
):
    rows, width = img_hbm.shape
    cuts = pieces_of(rows)
    n_cuts = len(cuts)
    other = {"i": "t", "t": "i"}
    size = {g: 2 ** len(dims[g]) for g in "it"}
    raw = {"i": raw_img, "t": raw_txt}
    unit = {"i": unit_img, "t": unit_txt}
    coef = {"i": coef_img, "t": coef_txt}
    acc = {"i": acc_img, "t": acc_txt}
    out = {"i": out_img, "t": out_txt}
    into = {"i": in_img, "t": in_txt}
    g_recv = {"i": gr_img, "t": gr_txt}
    c_recv = {"i": cr_img, "t": cr_txt}
    s_recv = {"i": sr_img, "t": sr_txt}
    g_send = {"i": sends.at[0], "t": sends.at[1]}
    s_send = {"i": sends.at[2], "t": sends.at[3]}
    l_send = sends.at[4]

    peers = [across(*CORE)] + [across(*d) for g in "it" for d in dims[g]]
    barrier = pltpu.get_barrier_semaphore()
    for peer in peers:
        pl.semaphore_signal(barrier, inc=1, device_id=peer, device_id_type=MESH)
    loads = [
        pltpu.make_async_copy(source, target.at[0], load.at[n])
        for n, (source, target) in enumerate([(txt_hbm, raw_txt), (img_hbm, raw_img)])
    ]
    for copy in loads:
        copy.start()
    for copy in loads:
        copy.wait()
    pl.semaphore_wait(barrier, len(peers))

    gather = {}

    def spread(g, slot, j, p):
        to = slot | 1 << j
        piece = pl.ds(*cuts[p])
        copy = pltpu.make_async_remote_copy(
            src_ref=raw[g].at[slot, piece],
            dst_ref=raw[g].at[to, piece],
            send_sem=g_send[g],
            recv_sem=g_recv[g].at[to * n_cuts + p],
            device_id=across(*dims[g][j]),
            device_id_type=MESH,
        )
        copy.start()
        gather[g, to, p] = copy

    def share(g, slot, piece):
        return pltpu.make_async_remote_copy(
            src_ref=raw[g].at[slot, piece],
            dst_ref=raw[g].at[size[g] + slot, piece],
            send_sem=g_send[g],
            recv_sem=c_recv[g].at[slot],
            device_id=across(*CORE),
            device_id_type=MESH,
        )

    levels = max(len(d) for d in dims.values())
    for p in range(n_cuts):
        for j in range(levels):
            for g in "ti":
                if j < len(dims[g]):
                    spread(g, 0, j, p)
    for g in "ti":
        share(g, 0, pl.ds(0, rows)).start()

    def normalize(g, slot, core):
        values = raw[g][core * size[g] + slot].astype(jnp.float32)
        unit[g][slot, core] = (values * inverse_norm(values)).astype(jnp.bfloat16)

    def partner(g, slot):
        share(g, slot, pl.ds(0, rows)).wait_recv()
        normalize(g, slot, 1)

    for g in "ti":
        normalize(g, 0, 0)
    for g in "ti":
        partner(g, 0)
    for level in range(1, levels + 1):
        slots = [
            (g, s)
            for s in reversed(range(1, max(size.values())))
            for g in "ti"
            if s < size[g] and s.bit_count() == level
        ]
        for p in range(n_cuts):
            for g, s in slots:
                gather[g, s, p].wait_recv()
                for j in range(top(s) + 1, len(dims[g])):
                    spread(g, s, j, p)
                share(g, s, pl.ds(*cuts[p])).start()
                if p == n_cuts - 1:
                    normalize(g, s, 0)
        for g, s in slots:
            partner(g, s)

    scale, shift = scale_ref[0], shift_ref[0]
    n_mine = {g: size[g] * rows for g in "it"}

    def logits(g, t):
        o = other[g]
        take_r = min(TILE // rows, size[g])
        take_c = min(TILE // rows // 2, size[o])
        n_r, n_c = take_r * rows, take_c * 2 * rows
        steps = size[o] // take_c
        if isinstance(t, int):
            r, c = t // steps * take_r, t % steps * take_c
            at_r, at_c = r * rows, c * 2 * rows
        else:
            r, c = lax.div(t, steps) * take_r, lax.rem(t, steps) * take_c
            at_r = pl.multiple_of(r * rows, n_r)
            at_c = pl.multiple_of(c * 2 * rows, n_c)
        left = unit[g][pl.ds(r, take_r), 0].reshape(n_r, width)
        right = unit[o][pl.ds(c, take_c)].reshape(n_c, width)
        value = lax.dot_general(
            left, right, (((1,), (1,)), ((), ())), preferred_element_type=jnp.float32
        )
        value = value * scale + shift
        weight = scale
        if not isinstance(t, int) or t == 0:
            a = lax.broadcasted_iota(jnp.int32, value.shape, 0) + at_r
            b = lax.broadcasted_iota(jnp.int32, value.shape, 1) + at_c
            match = (a == b) & (a < rows)
            value = jnp.where(match, -value, value)
            weight = jnp.where(match, -scale, scale)
        e = jnp.exp(value)
        coef[g][pl.ds(at_r, n_r), pl.ds(at_c, n_c)] = (weight * (e / (1.0 + e))).astype(
            jnp.bfloat16
        )
        if g == "i":
            terms = jnp.log1p(e)
            fold = terms[:, :128]
            for k in range(1, n_c // 128):
                fold = fold + terms[:, k * 128 : (k + 1) * 128]
            if isinstance(t, int) and t % steps == 0:
                loss_lanes[pl.ds(at_r, n_r), :] = fold
            else:
                loss_lanes[pl.ds(at_r, n_r), :] += fold

    def all_logits(g):
        o = other[g]
        count = -(-size[g] // (TILE // rows)) * -(-size[o] * 2 // (TILE // rows))
        if g == "i" and count > 4:
            loss_lanes[...] = jnp.zeros_like(loss_lanes)
        tiles(count, functools.partial(logits, g))

    scatter = {}

    def pass_on(g, s, p):
        piece = pl.ds(*cuts[p])
        copy = pltpu.make_async_remote_copy(
            src_ref=out[g].at[s, piece],
            dst_ref=into[g].at[s, piece],
            send_sem=s_send[g],
            recv_sem=s_recv[g].at[s * n_cuts + p],
            device_id=across(*dims[g][top(s)]),
            device_id_type=MESH,
        )
        copy.start()
        scatter[g, s, p] = copy

    def grads(g, upper):
        half = size[g] // 2
        base = half if upper else 0
        step = min(half, TILE // rows)
        o = other[g]

        def body(t):
            first = base + t * step
            here = first * rows
            if not isinstance(first, int):
                here = pl.multiple_of(here, step * rows)
            value = jnp.dot(
                coef[g][pl.ds(here, step * rows), :],
                unit[o][...].reshape(2 * n_mine[o], width),
                preferred_element_type=jnp.float32,
            ).reshape(step, rows, width)
            if upper:
                out[g][pl.ds(first, step)] = value.astype(jnp.bfloat16)
            else:
                acc[g][pl.ds(first, step)] = value

        tiles(half // step, body)
        if upper:
            for s in reversed(range(half, size[g])):
                for p in range(n_cuts):
                    pass_on(g, s, p)

    all_logits("t")
    grads("t", True)
    all_logits("i")
    grads("i", True)

    losses = {}

    def loss_on(s, value):
        loss_out[s] = value
        copy = pltpu.make_async_remote_copy(
            src_ref=loss_out.at[s],
            dst_ref=loss_in.at[s],
            send_sem=l_send,
            recv_sem=lr.at[s],
            device_id=across(*dims["i"][top(s)]),
            device_id_type=MESH,
        )
        copy.start()
        losses[s] = copy

    def loss_total(k):
        value = loss_acc[:, k * rows : (k + 1) * rows]
        for j in reversed(range(top(k) + 1 if k else 0, len(dims["i"]))):
            losses[k | 1 << j].wait_recv()
            value = value + loss_in[k | 1 << j]
        return value

    loss_acc[...] = jnp.sum(loss_lanes[...].T, axis=0, keepdims=True)
    for s in reversed(range(size["i"] // 2, size["i"])):
        loss_on(s, loss_acc[:, s * rows : (s + 1) * rows])
    grads("t", False)
    grads("i", False)

    def total(g, k, p):
        piece = pl.ds(*cuts[p])
        value = acc[g][k, piece]
        for j in reversed(range(top(k) + 1 if k else 0, len(dims[g]))):
            scatter[g, k | 1 << j, p].wait_recv()
            value = value + into[g][k | 1 << j, piece].astype(jnp.float32)
        return value

    order = sorted(
        [(k.bit_length() - len(dims[g]), g, k) for g in "it" for k in range(1, size[g] // 2)],
        key=lambda item: (-item[0], item[1] != "t", -item[2]),
    )
    for p in range(n_cuts):
        for _, g, k in order:
            out[g][k, pl.ds(*cuts[p])] = total(g, k, p).astype(jnp.bfloat16)
            pass_on(g, k, p)
    for k in reversed(range(1, size["i"] // 2)):
        loss_on(k, loss_total(k))

    for p in range(n_cuts):
        for g, result in (("t", gt_ref), ("i", gi_ref)):
            piece = pl.ds(*cuts[p])
            grad = total(g, 0, p)
            values = raw[g][0, piece].astype(jnp.float32)
            inverse = inverse_norm(values)
            unit_row = values * inverse
            along = jnp.sum(unit_row * grad, axis=-1, keepdims=True)
            result[piece, :] = inverse * (grad - unit_row * along)
    loss_ref[...] = loss_total(0)

    def drain(ref, sem):
        pltpu.make_async_remote_copy(
            src_ref=ref,
            dst_ref=ref,
            send_sem=sem,
            recv_sem=sem,
            device_id=across(*CORE),
            device_id_type=MESH,
        ).wait_send()

    for g in "it":
        drain(raw[g].at[pl.ds(0, 2 * size[g] - 1)], g_send[g])
        drain(out[g].at[pl.ds(1, size[g] - 1)], s_send[g])
    drain(loss_out.at[pl.ds(1, size["i"] - 1)], l_send)


def hand_out(gi_from, gt_from, loss_from, gi_ref, gt_ref, loss_ref, sems):
    pairs = ((gi_from, gi_ref), (gt_from, gt_ref), (loss_from, loss_ref))
    copies = [pltpu.make_async_copy(a, b, sems.at[n]) for n, (a, b) in enumerate(pairs)]
    for copy in copies:
        copy.start()
    for copy in copies:
        copy.wait()


def on_device(n_row, n_col, images, texts, scale, shift):
    rows, width = images.shape
    dims = dict(zip("it", groups(n_row, n_col)))
    a, b = 2 ** len(dims["i"]), 2 ** len(dims["t"])
    n_cuts = len(pieces_of(rows))
    vmem = pl.BlockSpec(memory_space=pltpu.VMEM)
    smem = pl.BlockSpec(memory_space=pltpu.SMEM)
    hbm = pl.BlockSpec(memory_space=pl.ANY)
    f32, bf16 = jnp.float32, jnp.bfloat16
    dma = pltpu.SemaphoreType.DMA
    sums = pl.pallas_call(
        functools.partial(kernel, dims),
        out_shape=(
            pltpu.VMEM((rows, width), f32),
            pltpu.VMEM((rows, width), f32),
            pltpu.VMEM((1, rows), f32),
        ),
        in_specs=[hbm, hbm, smem, smem],
        out_specs=(vmem, vmem, vmem),
        scratch_shapes=[
            pltpu.VMEM((2 * a, rows, width), bf16),
            pltpu.VMEM((2 * b, rows, width), bf16),
            pltpu.VMEM((a, 2, rows, width), bf16),
            pltpu.VMEM((b, 2, rows, width), bf16),
            pltpu.VMEM((a * rows, 2 * b * rows), bf16),
            pltpu.VMEM((b * rows, 2 * a * rows), bf16),
            pltpu.VMEM((a // 2, rows, width), f32),
            pltpu.VMEM((b // 2, rows, width), f32),
            pltpu.VMEM((a, rows, width), bf16),
            pltpu.VMEM((b, rows, width), bf16),
            pltpu.VMEM((a, rows, width), bf16),
            pltpu.VMEM((b, rows, width), bf16),
            pltpu.VMEM((a * rows, 128), f32),
            pltpu.VMEM((1, a * rows), f32),
            pltpu.VMEM((a, 1, rows), f32),
            pltpu.VMEM((a, 1, rows), f32),
            dma((2,)),
            dma((5,)),
            dma((a * n_cuts,)),
            dma((b * n_cuts,)),
            dma((a,)),
            dma((b,)),
            dma((a * n_cuts,)),
            dma((b * n_cuts,)),
            dma((a,)),
        ],
        compiler_params=pltpu.CompilerParams(collective_id=0, has_side_effects=True),
    )(*[pltpu.with_memory_space_constraint(x, pltpu.HBM) for x in (images, texts)], scale, shift)
    gi, gt, loss = pl.pallas_call(
        hand_out,
        out_shape=(
            jax.ShapeDtypeStruct((rows, width), f32),
            jax.ShapeDtypeStruct((rows, width), f32),
            jax.ShapeDtypeStruct((1, rows), f32),
        ),
        in_specs=[hbm] * 3,
        out_specs=(hbm, hbm, hbm),
        scratch_shapes=[pltpu.SemaphoreType.DMA((3,))],
    )(*[pltpu.with_memory_space_constraint(x, pltpu.VMEM) for x in sums])
    return gi, gt, loss.reshape(rows)


def solution(mesh):
    placed = (P(("row", "col"), None), P(("row", "col"), None), P(), P())
    return jax.shard_map(
        functools.partial(on_device, mesh.shape["row"], mesh.shape["col"]),
        mesh=mesh,
        in_specs=placed,
        out_specs=(P(("row", "col"), None), P(("row", "col"), None), P(("row", "col"))),
        check_vma=False,
    )
```

time: 34.9 us -> 33.7 us (0.966)
  Pallas kernels: 32.8 us -> 31.6 us
    pallas_call x1, Pallas kernels: 32 us -> 30.8 us  [on_device(): pl.pallas_call(functools.partial(kernel, dims), out_shape=(pltpu.VMEM((ro...]
where the time goes in v1:
time: 33.7 us; the launch traced here: 33.5 us
  Pallas kernels  31.6 us (94%)
  between operations  1.93 us (6%)
    pallas_call x1, Pallas kernels, on_device(): pl.pallas_call(functools.partial(kernel, dims), out_shape=(pltpu.VMEM((ro...  30.8 us
    pallas_call x1, Pallas kernels, on_device(): pl.pallas_call(hand_out, out_shape=(jax.ShapeDtypeStruct((rows, width), f...  0.84 us

profile of v1, /device:TPU:0, one launch (start us, length us, event | category | flops | bytes accessed | tf_op | source)
XLA Modules:
  0.0 33.5 jit_solution(12845632079150785599)
XLA Ops:
  1.9 30.8 %shard_map.67 = (f32[64,1152]{1,0:T(8,128)S(1)}, f32[64,1152]{1,0:T(8,128)S(1)}, f32[1,64]{1,0:T(1,128)S(1)}) custom-call(bf16[64,1152]{1,0:T(8,128)(2,1)} %img_hbm.1, bf16[64,1152]{1,0:T(8,128)(2,1)} %txt_hbm.1, f32[1]{0:T(128)S(6)} %copy.7.scale_ref, f32[1]{0:T(128)S(6)} %copy.8.shift_ref), custom_call_target="tpu_custom_call" | custom-call | tf_op jit(solution)/shard_map/pallas_call | solution.py:385
  32.7 0.8 %shard_map.68 = (f32[64,1152]{1,0:T(8,128)}, f32[64,1152]{1,0:T(8,128)}, f32[1,64]{1,0:T(1,128)}) custom-call(f32[64,1152]{1,0:T(8,128)S(1)} %get-tuple-element.9.gi_from, f32[64,1152]{1,0:T(8,128)S(1)} %get-tuple-element.10.gt_from, f32[1,64]{1,0:T(1,128)S(1)} %get-tuple-element.11.loss_from), custom_call_target="tpu_custom_call" | custom-call | tf_op jit(solution)/shard_map/pallas_call | solution.py:423

commit v2 on v1

v2 whole, which is shorter than its diff:
```python
import functools
import heapq

import jax
import jax.numpy as jnp
from jax import lax
from jax.experimental import pallas as pl
from jax.experimental.pallas import tpu as pltpu
from jax.sharding import PartitionSpec as P

EPS = 1e-06
MESH = pl.DeviceIdType.MESH
CORE = ("row", 0)
TILE = 256


def bits_of(n):
    return n.bit_length() - 1


def groups(n_row, n_col):
    row_bits, col_bits = bits_of(n_row), bits_of(n_col)
    take = min(max((row_bits + col_bits + 1) // 2 - row_bits, 0), col_bits)
    choice = [b for b in range(1, col_bits)] + [0] * (col_bits > 0)
    mine, rest = choice[:take], choice[take:]
    images = [("row", b) for b in range(1, row_bits)] + [("col", b) for b in sorted(mine)]
    texts = [("col", b) for b in sorted(rest)]
    return images, texts


def flip(index, bit):
    step = 2**bit
    return index + step * (1 - 2 * lax.rem(lax.div(index, step), 2))


def across(axis, bit):
    at = {"row": lax.axis_index("row"), "col": lax.axis_index("col")}
    at[axis] = flip(at[axis], bit)
    return (at["row"], at["col"])


def cuts_of(rows):
    quarter = rows // 4
    return [(p * quarter, quarter) for p in range(4)]


def order_of(n_dims, p):
    return list(range(n_dims)) if p == 3 else list(reversed(range(n_dims)))


def last_bit(slot, order):
    return [j for j in order if slot >> j & 1][-1]


def later(slot, order):
    return order[order.index(last_bit(slot, order)) + 1 :] if slot else order


def expected(nodes):
    ready = [(0, rank, key) for key, (_, _, deps, rank) in nodes.items() if not deps]
    heapq.heapify(ready)
    users = {}
    for key, (_, _, deps, _) in nodes.items():
        for dep in deps:
            users.setdefault(dep, []).append(key)
    free, arrival = {}, {}
    while ready:
        at, _, key = heapq.heappop(ready)
        link, latency, _, _ = nodes[key]
        free[link] = max(at, free.get(link, 0)) + (1 if link else 0)
        arrival[key] = max(at, free[link]) + latency
        for user in users.get(key, []):
            _, _, deps, rank = nodes[user]
            if all(d in arrival for d in deps):
                heapq.heappush(ready, (max(arrival[d] for d in deps), rank, user))
    return arrival


def link_of(dim):
    axis, bit = dim
    return (axis, axis == "col" and bit > 0), 2 + (axis == "col" and bit > 1)


def inverse_norm(values):
    return lax.rsqrt(jnp.sum(values * values, axis=-1, keepdims=True) + EPS)


def tiles(count, body):
    if count <= 4:
        for t in range(count):
            body(t)
    else:
        lax.fori_loop(0, count, lambda t, _: (body(t), 0)[1], 0)


def kernel(
    dims,
    img_hbm,
    txt_hbm,
    scale_ref,
    shift_ref,
    gi_ref,
    gt_ref,
    loss_ref,
    raw_img,
    raw_txt,
    unit_img,
    unit_txt,
    coef_img,
    coef_txt,
    acc_img,
    acc_txt,
    out_img,
    out_txt,
    in_img,
    in_txt,
    loss_lanes,
    loss_acc,
    loss_out,
    loss_in,
    load,
    sends,
    gr_img,
    gr_txt,
    cr_img,
    cr_txt,
    sr_img,
    sr_txt,
    lr,
):
    rows, width = img_hbm.shape
    cuts = cuts_of(rows)
    n_cuts = len(cuts)
    other = {"i": "t", "t": "i"}
    size = {g: 2 ** len(dims[g]) for g in "it"}
    order = {g: [order_of(len(dims[g]), p) for p in range(n_cuts)] for g in "it"}
    raw = {"i": raw_img, "t": raw_txt}
    unit = {"i": unit_img, "t": unit_txt}
    coef = {"i": coef_img, "t": coef_txt}
    acc = {"i": acc_img, "t": acc_txt}
    out = {"i": out_img, "t": out_txt}
    into = {"i": in_img, "t": in_txt}
    g_recv = {"i": gr_img, "t": gr_txt}
    c_recv = {"i": cr_img, "t": cr_txt}
    s_recv = {"i": sr_img, "t": sr_txt}
    g_send = {"i": sends.at[0], "t": sends.at[1]}
    c_send = {"i": sends.at[2], "t": sends.at[3]}
    s_send = {"i": sends.at[4], "t": sends.at[5]}
    l_send = sends.at[6]

    peers = [across(*CORE)] + [across(*d) for g in "it" for d in dims[g]]
    barrier = pltpu.get_barrier_semaphore()
    for peer in peers:
        pl.semaphore_signal(barrier, inc=1, device_id=peer, device_id_type=MESH)
    loads = [
        pltpu.make_async_copy(source, target.at[0], load.at[n])
        for n, (source, target) in enumerate([(txt_hbm, raw_txt), (img_hbm, raw_img)])
    ]
    for copy in loads:
        copy.start()
    for copy in loads:
        copy.wait()
    pl.semaphore_wait(barrier, len(peers))

    gather = {}
    keys = [(g, s, p) for g in "ti" for s in range(1, size[g]) for p in range(n_cuts)]

    def spread(g, to, p):
        j = last_bit(to, order[g][p])
        piece = pl.ds(*cuts[p])
        copy = pltpu.make_async_remote_copy(
            src_ref=raw[g].at[to ^ 1 << j, piece],
            dst_ref=raw[g].at[to, piece],
            send_sem=g_send[g],
            recv_sem=g_recv[g].at[(to - 1) * n_cuts + p],
            device_id=across(*dims[g][j]),
            device_id_type=MESH,
        )
        copy.start()
        gather[g, to, p] = copy

    def share(g, slot, piece):
        return pltpu.make_async_remote_copy(
            src_ref=unit[g].at[slot, 0, piece],
            dst_ref=unit[g].at[slot, 1, piece],
            send_sem=c_send[g],
            recv_sem=c_recv[g].at[slot],
            device_id=across(*CORE),
            device_id_type=MESH,
        )

    def normalize(g, slot, piece):
        values = raw[g][slot, piece].astype(jnp.float32)
        unit[g][slot, 0, piece] = (values * inverse_norm(values)).astype(jnp.bfloat16)
        share(g, slot, piece).start()

    nodes = {}
    for g, to, p in keys:
        j = last_bit(to, order[g][p])
        rest = to ^ 1 << j
        rank = (order[g][p].index(j), p, g == "i")
        nodes[g, to, p] = (*link_of(dims[g][j]), [(g, rest, p)] if rest else [], rank)
    arrival = expected(nodes)
    for g, to, p in sorted(keys, key=lambda key: nodes[key][3]):
        if to.bit_count() == 1:
            spread(g, to, p)
    for g in "ti":
        normalize(g, 0, pl.ds(0, rows))

    def partner(slot):
        for g in "it":
            if slot < size[g]:
                share(g, slot, pl.ds(0, rows)).wait_recv()

    scale, shift = scale_ref[0], shift_ref[0]
    n_mine = {g: size[g] * rows for g in "it"}

    def tile(g, r, take_r, c, take_c):
        o = other[g]
        n_r, n_c = take_r * rows, take_c * 2 * rows
        at_r, at_c = r * rows, c * 2 * rows
        fixed = isinstance(r, int)
        if not fixed:
            at_r, at_c = pl.multiple_of(at_r, n_r), pl.multiple_of(at_c, n_c)
        left = unit[g][pl.ds(r, take_r), 0].reshape(n_r, width)
        right = unit[o][pl.ds(c, take_c)].reshape(n_c, width)
        value = lax.dot_general(
            left, right, (((1,), (1,)), ((), ())), preferred_element_type=jnp.float32
        )
        value = value * scale + shift
        weight = scale
        if not fixed or (r == 0 and c == 0):
            a = lax.broadcasted_iota(jnp.int32, value.shape, 0) + at_r
            b = lax.broadcasted_iota(jnp.int32, value.shape, 1) + at_c
            match = (a == b) & (a < rows)
            value = jnp.where(match, -value, value)
            weight = jnp.where(match, -scale, scale)
        e = jnp.exp(value)
        here = pl.ds(at_r, n_r)
        coef[g][here, pl.ds(at_c, n_c)] = (weight * (e / (1.0 + e))).astype(jnp.bfloat16)
        if g == "i":
            terms = jnp.log1p(e)
            fold = terms[:, :128]
            for k in range(1, n_c // 128):
                fold = fold + terms[:, k * 128 : (k + 1) * 128]
            if fixed and c == 0:
                loss_lanes[here, :] = fold
            else:
                loss_lanes[here, :] += fold

    def all_tiles(g):
        take_r, take_c = min(TILE // rows, size[g]), min(TILE // rows // 2, size[other[g]])
        n_c = size[other[g]] // take_c
        if g == "i":
            loss_lanes[...] = jnp.zeros_like(loss_lanes)
        lax.fori_loop(
            0,
            size[g] // take_r * n_c,
            lambda t, _: (
                tile(g, lax.div(t, n_c) * take_r, take_r, lax.rem(t, n_c) * take_c, take_c),
                0,
            )[1],
            0,
        )

    stream = size["i"] == size["t"] == 4
    steps = {}
    if stream:
        steps[1, True] = [("t", 0, 2, 0, 2), ("i", 0, 2, 0, 2)]
        steps[2, True] = [(g, *at) for g in "ti" for at in ((2, 1, 0, 3), (0, 2, 2, 1))]
        steps[3, False] = [(g, 3, 1, 0, 3) for g in "ti"]
        steps[3, True] = [(g, 0, 4, 3, 1) for g in "ti"]
    left = {s: sum(key[1] == s for key in keys) for s in range(1, max(size.values()))}
    waiting = [0]

    def partners():
        for s in waiting:
            partner(s)
            for args in steps.get((s, True), []):
                tile(*args)
        waiting.clear()

    for g, s, p in sorted(keys, key=lambda key: (arrival[key], nodes[key][3])):
        gather[g, s, p].wait_recv()
        for j in later(s, order[g][p]):
            spread(g, s | 1 << j, p)
        normalize(g, s, pl.ds(*cuts[p]))
        left[s] -= 1
        if left[s] == 0:
            partners()
            for args in steps.get((s, False), []):
                tile(*args)
            waiting.append(s)
    partners()
    if not stream:
        all_tiles("t")
        all_tiles("i")

    scatter = {}

    def pass_on(g, s, p):
        piece = pl.ds(*cuts[p])
        copy = pltpu.make_async_remote_copy(
            src_ref=out[g].at[s, piece],
            dst_ref=into[g].at[s, piece],
            send_sem=s_send[g],
            recv_sem=s_recv[g].at[(s - 1) * n_cuts + p],
            device_id=across(*dims[g][last_bit(s, order[g][p])]),
            device_id_type=MESH,
        )
        copy.start()
        scatter[g, s, p] = copy

    def at_once(g, s, p):
        return s > 0 and not later(s, order[g][p])

    def grads(g, first, count):
        o = other[g]
        step = min(count, TILE // rows)

        def body(t):
            slot = first + t * step
            here = slot * rows
            if not isinstance(slot, int):
                here = pl.multiple_of(here, step * rows)
            value = jnp.dot(
                coef[g][pl.ds(here, step * rows), :],
                unit[o][...].reshape(2 * size[o] * rows, width),
                preferred_element_type=jnp.float32,
            ).reshape(step, rows, width)
            if not isinstance(slot, int):
                acc[g][pl.ds(slot, step)] = value
                out[g][pl.ds(slot, step)] = value.astype(jnp.bfloat16)
                return
            for k in range(step):
                for p, (start, length) in enumerate(cuts):
                    piece = pl.ds(start, length)
                    part = value[k, start : start + length]
                    if at_once(g, slot + k, p):
                        out[g][slot + k, piece] = part.astype(jnp.bfloat16)
                    else:
                        acc[g][slot + k, piece] = part

        tiles(count // step, body)
        for s in reversed(range(first, first + count)):
            for p in range(n_cuts):
                if at_once(g, s, p):
                    pass_on(g, s, p)

    losses = {}
    l_order = order["i"][0]

    def loss_on(s, value):
        loss_out[s] = value
        copy = pltpu.make_async_remote_copy(
            src_ref=loss_out.at[s],
            dst_ref=loss_in.at[s],
            send_sem=l_send,
            recv_sem=lr.at[s - 1],
            device_id=across(*dims["i"][last_bit(s, l_order)]),
            device_id_type=MESH,
        )
        copy.start()
        losses[s] = copy

    def loss_total(k):
        value = loss_acc[:, k * rows : (k + 1) * rows]
        for j in reversed(later(k, l_order)):
            losses[k | 1 << j].wait_recv()
            value = value + loss_in[k | 1 << j]
        return value

    l_later = sorted(
        range(1, size["i"]), key=lambda s: (-l_order.index(last_bit(s, l_order)), -s)
    )
    grads("t", size["t"] // 2, size["t"] // 2)
    loss_acc[...] = jnp.sum(loss_lanes[...].T, axis=0, keepdims=True)
    for s in l_later:
        if not later(s, l_order):
            loss_on(s, loss_acc[:, s * rows : (s + 1) * rows])
    grads("i", size["i"] // 2, size["i"] // 2)
    grads("t", 0, size["t"] // 2)
    grads("i", 0, size["i"] // 2)

    def total(g, k, p):
        piece = pl.ds(*cuts[p])
        value = acc[g][k, piece]
        for j in reversed(later(k, order[g][p])):
            scatter[g, k | 1 << j, p].wait_recv()
            value = value + into[g][k | 1 << j, piece].astype(jnp.float32)
        return value

    nodes = {}
    for g, s, p in keys + [(g, 0, p) for g in "ti" for p in range(n_cuts)]:
        deps = [(g, s | 1 << j, p) for j in later(s, order[g][p])]
        link = link_of(dims[g][last_bit(s, order[g][p])]) if s else (None, 0)
        nodes[g, s, p] = (*link, deps, (-s, p, g == "i"))
    arrival = expected(nodes)
    due = {
        key: (max(arrival[d] for d in deps), rank)
        for key, (_, _, deps, rank) in nodes.items()
        if deps
    }
    result = {"i": gi_ref, "t": gt_ref}
    for g, k, p in sorted(due, key=due.get):
        piece = pl.ds(*cuts[p])
        if k:
            out[g][k, piece] = total(g, k, p).astype(jnp.bfloat16)
            pass_on(g, k, p)
            continue
        if l_later:
            for s in l_later:
                if later(s, l_order):
                    loss_on(s, loss_total(s))
            l_later.clear()
        grad = total(g, 0, p)
        values = raw[g][0, piece].astype(jnp.float32)
        inverse = inverse_norm(values)
        along = jnp.sum(values * grad, axis=-1, keepdims=True)
        result[g][piece, :] = inverse * (grad - values * (inverse * inverse * along))
    loss_ref[...] = loss_total(0)

    def drain(ref, sem):
        pltpu.make_async_remote_copy(
            src_ref=ref,
            dst_ref=ref,
            send_sem=sem,
            recv_sem=sem,
            device_id=across(*CORE),
            device_id_type=MESH,
        ).wait_send()

    for g in "it":
        drain(raw[g].at[pl.ds(1, size[g] - 1)], g_send[g])
        drain(unit[g].at[pl.ds(0, size[g]), 0], c_send[g])
        drain(out[g].at[pl.ds(1, size[g] - 1)], s_send[g])
    drain(loss_out.at[pl.ds(1, size["i"] - 1)], l_send)


def hand_out(gi_from, gt_from, loss_from, gi_ref, gt_ref, loss_ref, sems):
    pairs = ((gi_from, gi_ref), (gt_from, gt_ref), (loss_from, loss_ref))
    copies = [pltpu.make_async_copy(a, b, sems.at[n]) for n, (a, b) in enumerate(pairs)]
    for copy in copies:
        copy.start()
    for copy in copies:
        copy.wait()


def on_device(n_row, n_col, images, texts, scale, shift):
    rows, width = images.shape
    dims = dict(zip("it", groups(n_row, n_col)))
    a, b = 2 ** len(dims["i"]), 2 ** len(dims["t"])
    n_cuts = len(cuts_of(rows))
    vmem = pl.BlockSpec(memory_space=pltpu.VMEM)
    smem = pl.BlockSpec(memory_space=pltpu.SMEM)
    hbm = pl.BlockSpec(memory_space=pl.ANY)
    f32, bf16 = jnp.float32, jnp.bfloat16
    dma = pltpu.SemaphoreType.DMA
    sums = pl.pallas_call(
        functools.partial(kernel, dims),
        out_shape=(
            pltpu.VMEM((rows, width), f32),
            pltpu.VMEM((rows, width), f32),
            pltpu.VMEM((1, rows), f32),
        ),
        in_specs=[hbm, hbm, smem, smem],
        out_specs=(vmem, vmem, vmem),
        scratch_shapes=[
            pltpu.VMEM((a, rows, width), bf16),
            pltpu.VMEM((b, rows, width), bf16),
            pltpu.VMEM((a, 2, rows, width), bf16),
            pltpu.VMEM((b, 2, rows, width), bf16),
            pltpu.VMEM((a * rows, 2 * b * rows), bf16),
            pltpu.VMEM((b * rows, 2 * a * rows), bf16),
            pltpu.VMEM((a, rows, width), f32),
            pltpu.VMEM((b, rows, width), f32),
            pltpu.VMEM((a, rows, width), bf16),
            pltpu.VMEM((b, rows, width), bf16),
            pltpu.VMEM((a, rows, width), bf16),
            pltpu.VMEM((b, rows, width), bf16),
            pltpu.VMEM((a * rows, 128), f32),
            pltpu.VMEM((1, a * rows), f32),
            pltpu.VMEM((a, 1, rows), f32),
            pltpu.VMEM((a, 1, rows), f32),
            dma((2,)),
            dma((7,)),
            dma(((a - 1) * n_cuts,)),
            dma(((b - 1) * n_cuts,)),
            dma((a,)),
            dma((b,)),
            dma(((a - 1) * n_cuts,)),
            dma(((b - 1) * n_cuts,)),
            dma((a - 1,)),
        ],
        compiler_params=pltpu.CompilerParams(collective_id=0, has_side_effects=True),
    )(*[pltpu.with_memory_space_constraint(x, pltpu.HBM) for x in (images, texts)], scale, shift)
    gi, gt, loss = pl.pallas_call(
        hand_out,
        out_shape=(
            jax.ShapeDtypeStruct((rows, width), f32),
            jax.ShapeDtypeStruct((rows, width), f32),
            jax.ShapeDtypeStruct((1, rows), f32),
        ),
        in_specs=[hbm] * 3,
        out_specs=(hbm, hbm, hbm),
        scratch_shapes=[pltpu.SemaphoreType.DMA((3,))],
    )(*[pltpu.with_memory_space_constraint(x, pltpu.VMEM) for x in sums])
    return gi, gt, loss.reshape(rows)


def solution(mesh):
    placed = (P(("row", "col"), None), P(("row", "col"), None), P(), P())
    return jax.shard_map(
        functools.partial(on_device, mesh.shape["row"], mesh.shape["col"]),
        mesh=mesh,
        in_specs=placed,
        out_specs=(P(("row", "col"), None), P(("row", "col"), None), P(("row", "col"))),
        check_vma=False,
    )
```

time: 33.7 us -> 31.5 us (0.935)
  Pallas kernels: 31.6 us -> 29.4 us
    pallas_call x1, Pallas kernels: 30.8 us -> 28.6 us  [on_device(): pl.pallas_call(functools.partial(kernel, dims), out_shape=(pltpu.VMEM((ro...]
where the time goes in v2:
time: 31.5 us; the launch traced here: 31.4 us
  Pallas kernels  29.4 us (93%)
  between operations  1.93 us (6%)
    pallas_call x1, Pallas kernels, on_device(): pl.pallas_call(functools.partial(kernel, dims), out_shape=(pltpu.VMEM((ro...  28.6 us
    pallas_call x1, Pallas kernels, on_device(): pl.pallas_call(hand_out, out_shape=(jax.ShapeDtypeStruct((rows, width), f...  0.84 us

profile of v2, /device:TPU:0, one launch (start us, length us, event | category | flops | bytes accessed | tf_op | source)
XLA Modules:
  0.0 31.4 jit_solution(6260148427921676511)
XLA Ops:
  1.9 28.6 %shard_map.67 = (f32[64,1152]{1,0:T(8,128)S(1)}, f32[64,1152]{1,0:T(8,128)S(1)}, f32[1,64]{1,0:T(1,128)S(1)}) custom-call(bf16[64,1152]{1,0:T(8,128)(2,1)} %img_hbm.1, bf16[64,1152]{1,0:T(8,128)(2,1)} %txt_hbm.1, f32[1]{0:T(128)S(6)} %copy.7.scale_ref, f32[1]{0:T(128)S(6)} %copy.8.shift_ref), custom_call_target="tpu_custom_call" | custom-call | tf_op jit(solution)/shard_map/pallas_call | solution.py:459
  30.5 0.8 %shard_map.68 = (f32[64,1152]{1,0:T(8,128)}, f32[64,1152]{1,0:T(8,128)}, f32[1,64]{1,0:T(1,128)}) custom-call(f32[64,1152]{1,0:T(8,128)S(1)} %get-tuple-element.9.gi_from, f32[64,1152]{1,0:T(8,128)S(1)} %get-tuple-element.10.gt_from, f32[1,64]{1,0:T(1,128)S(1)} %get-tuple-element.11.loss_from), custom_call_target="tpu_custom_call" | custom-call | tf_op jit(solution)/shard_map/pallas_call | solution.py:497
